TPU v7x, 32 devices: a whole 2x2x4 slice. The times are simulated.
32 devices in a mesh: gx: 4 (over z), gy: 8 (over y, x, core).
Axes of the slice: x: 2, y: 2, z: 4, core: 2. Of those that a mesh axis runs over, the one named last changes fastest.
Arguments:
- density: float32 [8, 512, 2048], P(None, 'gy', 'gx'), may hold values from -6 to 6
- tracer: float32 [8, 512, 2048], P(None, 'gy', 'gx'), may hold values from -6 to 6
- sea_mask: int32 [512, 2048], P('gy', 'gx'), may hold values 0 or 1
- mixed_level: int32 [512, 2048], P('gy', 'gx'), may hold values from 0 to 4
- tile_blocks: int32 [64], replicated, may hold values from 0 to 63, each once
- block_owner: int32 [64], replicated, may hold values from 0 to 63, as said below
Outputs:
- tracer_out: float32 [8, 512, 2048], P(None, 'gy', 'gx')
Inputs may be any that keep to these rules, and one draw needn't show every extreme that they name: `sea_mask`: 1 marks sea, 0 land. `tile_blocks`: each of the 64 blocks once. `block_owner`: each of the 64 dynamics slots once; slot t belongs to gy index t // 8; of the 8 physics slots of one gy index, at most 2 go to any one gy index, and exactly 2 to every gy index that they reach.
All inputs are finite; a program needn't handle non-finite values. No bound on the sum of `sea_mask` on one device may be relied on, other than what follows from the above.
Results may differ from a plain program's by a relative error of at most 0.0003.
Values sent between devices are 32-bit elements; how exact they have to be, the bound alone decides.
A program may use at most 128 MiB of HBM per device.

v0:
```python
import functools

import jax
import jax.numpy as jnp
from jax import lax
from jax.experimental import pallas as pl
from jax.experimental.pallas import tpu as pltpu
from jax.sharding import PartitionSpec as P

BR = 8
BPD = 8
ITERS = 4
EDGE = 8
LANES = 128
EROWS = 16

TIME_STEP = 0.2
STRATIFICATION = 1.0
DENSITY_FLOOR = 0.25
SLOPE_LIMIT = 1.0
TAPER_WIDTH = 0.5
KERNEL_OFFSET = 0.05
BASE_DIFFUSIVITY = 0.2
VISBECK_ALPHA = 0.5

MESH = pl.DeviceIdType.MESH


def pack_kernel(levels, dl, dr, tl, tr, ml, mr, xl, xr, left_ref, right_ref):
    lane = lax.broadcasted_iota(jnp.int32, (BR, LANES), 1)
    row = lax.broadcasted_iota(jnp.int32, (BR, LANES), 0)

    def one(tile, shift, keep):
        tile = jnp.where(keep, tile, 0.0)
        tile = pltpu.roll(tile, (shift + (BR - 1) * EDGE) % LANES, 1)
        for bit in (1, 2, 4):
            tile = jnp.where((row & bit) > 0, pltpu.roll(tile, LANES - bit * EDGE, 1), tile)
        return jnp.sum(tile, axis=0, keepdims=True)

    def side(b, d, t, m, x, out_ref, base, keep):
        tiles = [d[k, b] for k in range(levels)]
        tiles += [m[b].astype(jnp.float32), x[b].astype(jnp.float32)]
        tiles += [t[k, b] for k in range(levels)]
        half = LANES // 2
        rows = [
            one(tiles[2 * j], base, keep) + one(tiles[2 * j + 1], base + half, keep)
            for j in range(levels + 1)
        ]
        rows.append(jnp.zeros((EROWS - levels - 1, LANES), jnp.float32))
        out_ref[b] = jnp.concatenate(rows, axis=0)

    @pl.loop(0, BPD)
    def _(b):
        side(b, dl, tl, ml, xl, left_ref, 0, lane < EDGE)
        side(b, dr, tr, mr, xr, right_ref, EDGE, lane >= LANES - EDGE)


def pack_edges(density, tracer, sea, mixed):
    levels = density.shape[0]
    last = density.shape[-1] // LANES - 1
    big = lambda at: pl.BlockSpec((levels, BPD, BR, LANES), lambda i: (0, 0, 0, at))
    flat = lambda at: pl.BlockSpec((BPD, BR, LANES), lambda i: (0, 0, at))
    whole = pl.BlockSpec((BPD, EROWS, LANES), lambda i: (0, 0, 0))
    shape = jax.ShapeDtypeStruct((BPD, EROWS, LANES), jnp.float32)
    return pl.pallas_call(
        functools.partial(pack_kernel, levels),
        grid=(1,),
        in_specs=[big(0), big(last), big(0), big(last), flat(0), flat(last), flat(0), flat(last)],
        out_specs=[whole, whole],
        out_shape=[shape, shape],
        name="pack_edges",
    )(density, density, tracer, tracer, sea, sea, mixed, mixed)


def gather_kernel(
    columns, d, m, x, t, left, right,
    gd, gm, gx, gt, gel, ger,
    vd, vm, vx, vt, in_sem, own_sem, z_send, z_recv, send_sem, recv_sem,
):
    me = lax.axis_index("gy")
    mx = lax.axis_index("gx")
    east = lax.rem(mx + 1, columns)
    west = lax.rem(mx + columns - 1, columns)

    def flip(bit):
        return me + bit - 2 * bit * lax.rem(me // bit, 2)

    core, ex, wy = flip(1), flip(2), flip(4)
    diag = flip(2) + flip(4) - me
    offset_core = core - me
    barrier = pltpu.get_barrier_semaphore()
    for peer in (core, ex, wy):
        pl.semaphore_signal(barrier, inc=1, device_id={"gy": peer}, device_id_type=MESH)
    for peer in (east, west):
        pl.semaphore_signal(barrier, inc=1, device_id={"gx": peer}, device_id_type=MESH)
    pl.semaphore_wait(barrier, 5)

    low = d.shape[0] // 2
    cut = lambda ref, h: ref.at[pl.ds(h * low, low)]
    part = lambda ref, h: (lambda slot: ref.at[slot, pl.ds(h * low, low)])
    whole = lambda ref: (lambda slot: ref.at[slot])
    pieces = [
        (cut(d, 0), cut(vd, 0), part(gd, 0), 0),
        (cut(d, 1), cut(vd, 1), part(gd, 1), 1),
        (m, vm, whole(gm), 0),
        (x, vx, whole(gx), 1),
        (cut(t, 0), cut(vt, 0), part(gt, 0), 0),
        (cut(t, 1), cut(vt, 1), part(gt, 1), 1),
        (None, None, whole(gel), 0),
        (None, None, whole(ger), 1),
    ]
    staged = {}
    for i, (src, dst, _, _) in enumerate(pieces):
        if src is not None:
            staged[i] = pltpu.make_async_copy(src, dst, in_sem.at[i])
            staged[i].start()
    z_copies = [
        pltpu.make_async_remote_copy(
            right, gel.at[me], z_send.at[0], z_recv.at[0],
            device_id={"gx": east}, device_id_type=MESH),
        pltpu.make_async_remote_copy(
            left, ger.at[me], z_send.at[1], z_recv.at[1],
            device_id={"gx": west}, device_id_type=MESH),
    ]
    for copy in z_copies:
        copy.start()

    sent = {}

    def send(i, kind, src, slot, peer):
        copy = pltpu.make_async_remote_copy(
            src, pieces[i][2](slot), send_sem.at[i, kind], recv_sem.at[i, kind],
            device_id={"gy": peer}, device_id_type=MESH)
        copy.start()
        sent[i, kind] = copy

    own = []
    for i, (src, stage, place, _) in enumerate(pieces):
        if src is None:
            z_copies[i - len(staged)].wait_recv()
            stage = place(me)
        else:
            staged[i].wait()
        send(i, 0, stage, me, ex)
        send(i, 1, stage, me, wy)
        send(i, 2, stage, me, core)
        if src is not None:
            keep = pltpu.make_async_copy(stage, place(me), own_sem.at[i])
            keep.start()
            own.append(keep)
    for i, (_, _, place, way) in enumerate(pieces):
        sent[i, 0].wait_recv()
        if way == 0:
            send(i, 3, place(ex), ex, wy)
        send(i, 4, place(ex), ex, core)
        sent[i, 1].wait_recv()
        if way == 1:
            send(i, 3, place(wy), wy, ex)
        send(i, 5, place(wy), wy, core)
    for i, (_, _, place, _) in enumerate(pieces):
        sent[i, 3].wait_recv()
        send(i, 6, place(diag), diag, core)
    for i in range(len(pieces)):
        for kind in (2, 4, 5, 6):
            sent[i, kind].wait_recv()
    for copy in sent.values():
        copy.wait_send()
    for copy in z_copies:
        copy.wait_send()
    for copy in own:
        copy.wait()


def gather_blocks(count, columns, density, sea, mixed, tracer, left, right):
    arrays = (density, sea, mixed, tracer, left, right)
    if count != 8:
        ring = [(i, (i + 1) % columns) for i in range(columns)]
        back = [((i + 1) % columns, i) for i in range(columns)]
        arrays = arrays[:4] + (lax.ppermute(right, "gx", ring), lax.ppermute(left, "gx", back))
        return tuple(lax.all_gather(a, "gy", axis=0) for a in arrays)
    hbm = pl.BlockSpec(memory_space=pl.ANY)
    dma = pltpu.SemaphoreType.DMA
    return pl.pallas_call(
        functools.partial(gather_kernel, columns),
        in_specs=[hbm] * 6,
        out_specs=[hbm] * 6,
        out_shape=[jax.ShapeDtypeStruct((count,) + a.shape, a.dtype) for a in arrays],
        scratch_shapes=[pltpu.VMEM(a.shape, a.dtype) for a in arrays[:4]]
        + [dma((8,)), dma((8,)), dma((2,)), dma((2,)), dma((8, 7)), dma((8, 7))],
        compiler_params=pltpu.CompilerParams(collective_id=0, has_side_effects=True),
        name="gather_blocks",
    )(*arrays)


def block_kernel(levels, width, slots, dslots, valid, *refs):
    d, m, x, t = refs[0:3], refs[3:6], refs[6:9], refs[9:12]
    pel, per, tel, ter = refs[12:15], refs[15:18], refs[18:21], refs[21:24]
    out, grid_ref, cur, ae_ref, an_ref, av_ref, col = refs[24:]
    j = pl.program_id(0)
    wide = width + LANES
    rows = 2 * BR
    rim = BR // 2
    lane = lax.broadcasted_iota(jnp.int32, (BR, LANES), 1)

    def edge_tile(l_ref, r_ref, ch):
        row, base = ch // 2, (ch % 2) * (LANES // 2)

        def spread(ref, to):
            line = jnp.broadcast_to(ref[0, 0, row : row + 1, :], (BR, LANES))
            shift = (to - base - (BR - 1) * EDGE) % LANES
            return pltpu.roll(line, shift, 1, stride=EDGE, stride_axis=0)

        return jnp.where(
            lane < EDGE,
            spread(r_ref, 0),
            jnp.where(lane >= LANES - EDGE, spread(l_ref, LANES - EDGE), 0.0),
        )

    for o in range(3):
        here = pl.ds(o * BR, BR)
        there = valid[3 * j + o].astype(jnp.float32)
        for k in range(levels):
            grid_ref[k, here, :width] = d[o][0, k, 0]
            grid_ref[k, here, width:] = edge_tile(pel[o], per[o], k)
        grid_ref[levels, here, :width] = m[o][0, 0].astype(jnp.float32) * there
        grid_ref[levels, here, width:] = edge_tile(pel[o], per[o], levels) * there
        grid_ref[levels + 1, here, :width] = x[o][0, 0].astype(jnp.float32)
        grid_ref[levels + 1, here, width:] = edge_tile(pel[o], per[o], levels + 1)
        first, size, at = ((rim, rim, 0), (0, BR, rim), (0, rim, rim + BR))[o]
        for k in range(levels):
            cur[k, at : at + size, :width] = t[o][0, k, 0, first : first + size, :]
            tile = edge_tile(tel[o], ter[o], levels + 2 + k)
            cur[k, at : at + size, width:] = tile[first : first + size]

    east = lambda f: pltpu.roll(f, wide - 1, 1)
    west = lambda f: pltpu.roll(f, 1, 1)
    north = lambda f: pltpu.roll(f, rows - 1, 0)
    south = lambda f: pltpu.roll(f, 1, 0)
    mid = lambda k: grid_ref[k, rim : rim + rows, :]
    up = lambda k: grid_ref[k, rim + 1 : rim + 1 + rows, :]
    down = lambda k: grid_ref[k, rim - 1 : rim - 1 + rows, :]

    sea = mid(levels)
    col[0] = sea * east(sea)
    col[1] = sea * west(sea)
    col[2] = sea * up(levels)
    col[3] = sea * down(levels)
    depth = mid(levels + 1)
    col[4] = 1.0 / (depth + 1.0)
    total = jnp.zeros((rows, wide), jnp.float32)
    for k in range(levels):
        c = mid(k)
        ge = 0.5 * ((east(c) - c) * col[0] + (c - west(c)) * col[1])
        gn = 0.5 * ((up(k) - c) * col[2] + (c - down(k)) * col[3])
        hi, lo = min(k + 1, levels - 1), max(k - 1, 0)
        den = jnp.maximum(
            0.5 * (mid(hi) - mid(lo)) + 0.5 * STRATIFICATION * (hi - lo), DENSITY_FLOOR)
        inv = 1.0 / den
        se = -ge * inv
        sn = -gn * inv
        q = se * se + sn * sn
        taper = 0.5 * (1.0 + jnp.tanh((SLOPE_LIMIT - q) * (1.0 / TAPER_WIDTH)))
        factor = taper * jnp.minimum(1.0, (k + 1.0) * col[4]) * mid(levels)
        se = se * factor
        sn = sn * factor
        sq = se * se + sn * sn
        ae_ref[k] = se
        an_ref[k] = sn
        av_ref[k] = sq
        kern = jnp.sqrt(den * (sq + KERNEL_OFFSET))
        total = total + jnp.where(mid(levels + 1) <= k, kern, 0.0)
    sea = mid(levels)
    diff = sea * (
        BASE_DIFFUSIVITY + VISBECK_ALPHA * total / (levels - mid(levels + 1)))
    for k in range(levels):
        ae_ref[k] = ae_ref[k] * diff
        an_ref[k] = an_ref[k] * diff
        av_ref[k] = av_ref[k] * (0.5 * diff)
    step = (0.5 * TIME_STEP) * sea
    col[4] = (diff + east(diff)) * step * col[0]
    col[5] = (diff + west(diff)) * step * col[1]
    col[6] = (diff + north(diff)) * step * col[2]
    col[7] = (diff + south(diff)) * step * col[3]
    col[8] = step

    def iterate(_, carry):
        before = None
        flux = None
        held = None
        for k in range(levels):
            c = cur[k]
            de = east(c) - c
            dw = west(de)
            dn = north(c) - c
            ds = south(dn)
            dv = cur[min(k + 1, levels - 1)] - cur[max(k - 1, 0)]
            f = (
                ae_ref[k] * (col[0] * de + col[1] * dw)
                + an_ref[k] * (col[2] * dn + col[3] * ds)
                + av_ref[k] * dv
            )
            u = c + ((col[4] * de - col[5] * dw) + (col[6] * dn - col[7] * ds))
            if k > 0:
                jump = f if before is None else f - before
                cur[k - 1] = held + col[8] * jump
            before, flux, held = flux, f, u
        cur[levels - 1] = held - col[8] * before
        return carry

    lax.fori_loop(0, ITERS, iterate, 0)
    for k in range(levels):
        out[k, 0] = cur[k, rim : rim + BR, :width]


def run_blocks(slots, dslots, valid, gd, gm, gx, gt, gel, ger):
    levels, width = gd.shape[1], gd.shape[-1]

    def five(which, o):
        def at(j, *pre):
            s = pre[which][3 * j + o]
            return (lax.div(s, BPD), 0, lax.rem(s, BPD), 0, 0)
        return pl.BlockSpec((1, levels, 1, BR, width), at)

    def four(which, o, shape):
        def at(j, *pre):
            s = pre[which][3 * j + o]
            return (lax.div(s, BPD), lax.rem(s, BPD), 0, 0)
        return pl.BlockSpec((1, 1) + shape, at)

    three = range(3)
    edges = (EROWS, LANES)
    specs = [five(0, o) for o in three]
    specs += [four(0, o, (BR, width)) for o in three] * 2
    specs += [five(1, o) for o in three]
    specs += [four(0, o, edges) for o in three] * 2
    specs += [four(1, o, edges) for o in three] * 2
    wide = width + LANES
    f32 = lambda *shape: pltpu.VMEM(shape, jnp.float32)
    return pl.pallas_call(
        functools.partial(block_kernel, levels, width),
        grid_spec=pltpu.PrefetchScalarGridSpec(
            num_scalar_prefetch=3,
            grid=(BPD,),
            in_specs=specs,
            out_specs=pl.BlockSpec((levels, 1, BR, width), lambda j, *pre: (0, j, 0, 0)),
            scratch_shapes=[
                f32(levels + 2, 3 * BR, wide),
                f32(levels, 2 * BR, wide),
                f32(levels, 2 * BR, wide),
                f32(levels, 2 * BR, wide),
                f32(levels, 2 * BR, wide),
                f32(9, 2 * BR, wide),
            ],
        ),
        out_shape=jax.ShapeDtypeStruct((levels, BPD, BR, width), jnp.float32),
        name="run_blocks",
    )(
        slots, dslots, valid,
        gd, gd, gd, gm, gm, gm, gx, gx, gx, gt, gt, gt,
        gel, gel, gel, ger, ger, ger, gel, gel, gel, ger, ger, ger,
    )


def plan(tile_blocks, block_owner):
    blocks = tile_blocks.shape[0]
    at = jnp.arange(blocks, dtype=jnp.int32)
    mine = lax.axis_index("gy") * BPD + jnp.arange(BPD, dtype=jnp.int32)
    ids = jnp.sum(jnp.where(block_owner[None] == mine[:, None], tile_blocks[None], 0), axis=1)
    near = ids[:, None] + jnp.arange(-1, 2, dtype=jnp.int32)[None]
    valid = ((near >= 0) & (near < blocks)).astype(jnp.int32)
    near = jnp.clip(near, 0, blocks - 1)
    hit = tile_blocks[None, None] == near[..., None]
    slots = jnp.sum(jnp.where(hit, at, 0), axis=-1)
    dslots = jnp.sum(jnp.where(hit, block_owner, 0), axis=-1)
    return slots.reshape(-1), dslots.reshape(-1), valid.reshape(-1)


def on_device(count, columns, density, tracer, sea_mask, mixed_level, tile_blocks, block_owner):
    levels, height, width = density.shape
    split = lambda a: a.reshape(a.shape[:-2] + (BPD, BR, width))
    slots, dslots, valid = plan(tile_blocks, block_owner)
    density, tracer, sea, mixed = map(split, (density, tracer, sea_mask, mixed_level))
    left, right = pack_edges(density, tracer, sea, mixed)
    gathered = gather_blocks(count, columns, density, sea, mixed, tracer, left, right)
    gd, gm, gx, gt, gel, ger = gathered
    out = run_blocks(slots, dslots, valid, gd, gm, gx, gt, gel, ger)
    return out.reshape(levels, height, width)


def solution(mesh):
    placed = (P(None, "gy", "gx"), P(None, "gy", "gx"), P("gy", "gx"), P("gy", "gx"), P(), P())
    return jax.shard_map(
        functools.partial(on_device, mesh.shape["gy"], mesh.shape["gx"]),
        mesh=mesh, in_specs=placed, out_specs=P(None, "gy", "gx"), check_vma=False,
    )
```

profile of v0, /device:TPU:0, one launch (start us, length us, event | category | flops | bytes accessed | tf_op | source)
XLA Modules:
  0.0 135.8 jit_solution(3654168378900440306)
XLA Ops:
  0.0 0.9 select_reduce_fusion
  0.9 0.1 fusion.3
  0.9 0.6 reshape.79.valid
  1.5 0.1 add_clamp_fusion
  1.6 0.1 copy.7
  1.7 0.9 fusion.1
  2.6 0.1 copy.9
  2.7 0.6 reshape.73.dslots
  3.3 0.1 copy.8
  3.3 0.7 reshape.72.slots
  4.0 4.4 %pack_edges.1 = (f32[8,16,128]{2,1,0:T(8,128)}, f32[8,16,128]{2,1,0:T(8,128)}) custom-call(f32[8,8,8,512]{3,2,1,0:T(8,128)} %bitcast.5, f32[8,8,8,512]{3,2,1,0:T(8,128)} %bitcast.6, f32[8,8,8,512]{3,2,1,0:T(8,128)} %bitcast.8, f32[8,8,8,512]{3,2,1,0:T(8,128)} %bitcast.9, s32[8,8,512]{2,1,0:T(8,128)} %bitcast.11, s32[8,8,512]{2,1,0:T(8,128)} %bitcast.12, ...), custom_call_target="tpu_custom_call" | custom-call | tf_op jit(solution)/shard_map/pack_edges/pallas_call | solution.py:65
  8.4 91.5 %gather_blocks.1 = (f32[8,8,8,8,512]{4,3,2,1,0:T(8,128)}, s32[8,8,8,512]{3,2,1,0:T(8,128)}, s32[8,8,8,512]{3,2,1,0:T(8,128)}, f32[8,8,8,8,512]{4,3,2,1,0:T(8,128...) custom-call(f32[8,8,8,512]{3,2,1,0:T(8,128)} %bitcast.7, s32[8,8,512]{2,1,0:T(8,128)} %bitcast.13, ...), custom_call_target="tpu_custom_call" | custom-call | tf_op jit(solution)/shard_map/gather_blocks/pallas_call | solution.py:183
  99.9 35.8 %run_blocks.1 = f32[8,8,8,512]{3,2,1,0:T(8,128)} custom-call(s32[24]{0:T(128)} %reshape.72.slots, s32[24]{0:T(128)} %reshape.73.dslots, s32[24]{0:T(128)} %reshape.79.valid, f32[8,8,8,8,512]{4,3,2,1,0:T(8,128)} %get-tuple-element.15.refs_0_.refs_1_.refs_2_, f32[8,8,8,8,512]{4,3,2,1,0:T(8,128)} %get-tuple-element.15.refs_0_.refs_1_.refs_2_, ...), custom_call_target="tpu_custom_call" | custom-call | tf_op jit(solution)/shard_map/run_blocks/pallas_call | solution.py:339
  (2 shorter events, 0.0 us)
where the time goes:
time: 136 us
  Pallas kernels  132 us (97%)
  local copies, waits for them, and re-layouts  2.06 us (2%)
  other arithmetic  1.92 us (1%)
    pallas_call x1, Pallas kernels, gather_blocks(): pl.pallas_call(functools.partial(gather_kernel, columns), in_specs=[hbm]...  91.5 us
    pallas_call x1, Pallas kernels, run_blocks(): pl.pallas_call(functools.partial(block_kernel, levels, width), grid_spec=...  35.8 us
    pallas_call x1, Pallas kernels, pack_edges(): pl.pallas_call(functools.partial(pack_kernel, levels), grid=(1,), in_spec...  4.44 us

commit v1 on v0

v1 whole, which is shorter than its diff:
```python
import functools

import jax
import jax.numpy as jnp
from jax import lax
from jax.experimental import pallas as pl
from jax.experimental.pallas import tpu as pltpu
from jax.sharding import PartitionSpec as P

BR = 8
BPD = 8
ITERS = 4
EDGE = 8
LANES = 128

TIME_STEP = 0.2
STRATIFICATION = 1.0
DENSITY_FLOOR = 0.25
SLOPE_LIMIT = 1.0
TAPER_WIDTH = 0.5
KERNEL_OFFSET = 0.05
BASE_DIFFUSIVITY = 0.2
VISBECK_ALPHA = 0.5

MESH = pl.DeviceIdType.MESH


def own_lane():
    return lax.broadcasted_iota(jnp.int32, (BR, LANES), 1)


def pack_edges(levels, d, m, x, t, left_ref, right_ref):
    lane = own_lane()
    row = lax.broadcasted_iota(jnp.int32, (BR, LANES), 0)
    end = d.shape[-1] - LANES

    def one(tile, shift, keep):
        tile = jnp.where(keep, tile, 0.0)
        tile = pltpu.roll(tile, (shift + (BR - 1) * EDGE) % LANES, 1)
        for bit in (1, 2, 4):
            tile = jnp.where((row & bit) > 0, pltpu.roll(tile, LANES - bit * EDGE, 1), tile)
        return jnp.sum(tile, axis=0, keepdims=True)

    def side(b, start, out_ref, base, keep):
        span = pl.ds(start, LANES)
        tiles = [d[k, b, :, span] for k in range(levels)]
        tiles += [m[b, :, span].astype(jnp.float32), x[b, :, span].astype(jnp.float32)]
        tiles += [t[k, b, :, span] for k in range(levels)]
        half = LANES // 2
        for j in range(levels + 1):
            out_ref[j, pl.ds(b, 1), :] = (
                one(tiles[2 * j], base, keep) + one(tiles[2 * j + 1], base + half, keep))

    def step(b, carry):
        side(b, 0, left_ref, 0, lane < EDGE)
        side(b, end, right_ref, EDGE, lane >= LANES - EDGE)
        return carry

    lax.fori_loop(0, BPD, step, 0)


def edge_tile(lane, l_row, r_row, ch):
    base = (ch % 2) * (LANES // 2)

    def spread(row, to):
        line = jnp.broadcast_to(row(ch // 2), (BR, LANES))
        shift = (to - base - (BR - 1) * EDGE) % LANES
        return pltpu.roll(line, shift, 1, stride=EDGE, stride_axis=0)

    return jnp.where(
        lane < EDGE,
        spread(r_row, 0),
        jnp.where(lane >= LANES - EDGE, spread(l_row, LANES - EDGE), 0.0),
    )


def shifts(rows, wide):
    east = lambda f: pltpu.roll(f, wide - 1, 1)
    west = lambda f: pltpu.roll(f, 1, 1)
    north = lambda f: pltpu.roll(f, rows - 1, 0)
    south = lambda f: pltpu.roll(f, 1, 0)
    return east, west, north, south


def physics_block(levels, width, get, l_row, r_row, there, grid_ref, ae_ref, an_ref, av_ref, col):
    wide = width + LANES
    rows = 2 * BR
    rim = BR // 2
    lane = own_lane()
    for o in range(3):
        here = pl.ds(o * BR, BR)
        for k in range(levels + 2):
            main = get(o, k)
            tile = edge_tile(lane, l_row(o), r_row(o), k)
            if k == levels:
                main, tile = main * there[o], tile * there[o]
            grid_ref[k, here, :width] = main
            grid_ref[k, here, width:] = tile

    east, west, north, south = shifts(rows, wide)
    mid = lambda k: grid_ref[k, rim : rim + rows, :]
    up = lambda k: grid_ref[k, rim + 1 : rim + 1 + rows, :]
    down = lambda k: grid_ref[k, rim - 1 : rim - 1 + rows, :]

    sea = mid(levels)
    col[0] = sea * east(sea)
    col[1] = sea * west(sea)
    col[2] = sea * up(levels)
    col[3] = sea * down(levels)
    depth = mid(levels + 1)
    col[4] = 1.0 / (depth + 1.0)
    total = jnp.zeros((rows, wide), jnp.float32)
    for k in range(levels):
        c = mid(k)
        ge = 0.5 * ((east(c) - c) * col[0] + (c - west(c)) * col[1])
        gn = 0.5 * ((up(k) - c) * col[2] + (c - down(k)) * col[3])
        hi, lo = min(k + 1, levels - 1), max(k - 1, 0)
        den = jnp.maximum(
            0.5 * (mid(hi) - mid(lo)) + 0.5 * STRATIFICATION * (hi - lo), DENSITY_FLOOR)
        inv = 1.0 / den
        se = -ge * inv
        sn = -gn * inv
        q = se * se + sn * sn
        taper = 0.5 * (1.0 + jnp.tanh((SLOPE_LIMIT - q) * (1.0 / TAPER_WIDTH)))
        factor = taper * jnp.minimum(1.0, (k + 1.0) * col[4]) * mid(levels)
        se = se * factor
        sn = sn * factor
        sq = se * se + sn * sn
        ae_ref[k] = se
        an_ref[k] = sn
        av_ref[k] = sq
        kern = jnp.sqrt(den * (sq + KERNEL_OFFSET))
        total = total + jnp.where(mid(levels + 1) <= k, kern, 0.0)
    sea = mid(levels)
    diff = sea * (
        BASE_DIFFUSIVITY + VISBECK_ALPHA * total / (levels - mid(levels + 1)))
    for k in range(levels):
        ae_ref[k] = ae_ref[k] * diff
        an_ref[k] = an_ref[k] * diff
        av_ref[k] = av_ref[k] * (0.5 * diff)
    step = (0.5 * TIME_STEP) * sea
    col[4] = (diff + east(diff)) * step * col[0]
    col[5] = (diff + west(diff)) * step * col[1]
    col[6] = (diff + north(diff)) * step * col[2]
    col[7] = (diff + south(diff)) * step * col[3]
    col[8] = step


def advance_block(levels, width, get, l_row, r_row, cur, ae_ref, an_ref, av_ref, col, put):
    wide = width + LANES
    rows = 2 * BR
    rim = BR // 2
    lane = own_lane()
    for o in range(3):
        first, size, at = ((rim, rim, 0), (0, BR, rim), (0, rim, rim + BR))[o]
        for k in range(levels):
            cur[k, at : at + size, :width] = get(o, k)[first : first + size]
            tile = edge_tile(lane, l_row(o), r_row(o), levels + 2 + k)
            cur[k, at : at + size, width:] = tile[first : first + size]
    east, west, north, south = shifts(rows, wide)

    def iterate(_, carry):
        before = None
        flux = None
        held = None
        for k in range(levels):
            c = cur[k]
            de = east(c) - c
            dw = west(de)
            dn = north(c) - c
            ds = south(dn)
            dv = cur[min(k + 1, levels - 1)] - cur[max(k - 1, 0)]
            f = (
                ae_ref[k] * (col[0] * de + col[1] * dw)
                + an_ref[k] * (col[2] * dn + col[3] * ds)
                + av_ref[k] * dv
            )
            u = c + ((col[4] * de - col[5] * dw) + (col[6] * dn - col[7] * ds))
            if k > 0:
                jump = f if before is None else f - before
                cur[k - 1] = held + col[8] * jump
            before, flux, held = flux, f, u
        cur[levels - 1] = held - col[8] * before
        return carry

    lax.fori_loop(0, ITERS, iterate, 0)
    for k in range(levels):
        put(k, cur[k, rim : rim + BR, :width])


def gathered_block(levels, blocks, codes, j, gd, gm, gx, gt, gel, ger):
    code = [codes[3 * j + o] for o in range(3)]
    pair = [lax.rem(c, blocks * blocks) for c in code]
    there = [lax.div(c, blocks * blocks).astype(jnp.float32) for c in code]

    def where(slot):
        return lax.div(slot, BPD), lax.rem(slot, BPD)

    phys = [where(lax.rem(p, blocks)) for p in pair]
    dyn = [where(lax.div(p, blocks)) for p in pair]

    def grid(o, k):
        dev, at = phys[o]
        if k < levels:
            return gd[dev, k, at]
        return (gm if k == levels else gx)[dev, at].astype(jnp.float32)

    def tracer(o, k):
        dev, at = dyn[o]
        return gt[dev, k, at]

    def row_of(ref, places):
        return lambda o: (lambda r: ref[places[o][0], r, pl.ds(places[o][1], 1), :])

    rows = [row_of(ref, places) for places in (phys, dyn) for ref in (gel, ger)]
    return there, grid, tracer, rows


def whole_kernel(
    columns, codes, d, m, x, t, out,
    gd, gm, gx, gt, gel, ger, left, right,
    grid_ref, cur, ae, an, av, col,
    in_sem, z_send, z_recv, send_sem, recv_sem,
):
    levels, width = d.shape[0], d.shape[-1]
    count = gd.shape[0]
    blocks = count * BPD
    me = lax.axis_index("gy")
    mx = lax.axis_index("gx")
    east = lax.rem(mx + 1, columns)
    west = lax.rem(mx + columns - 1, columns)

    def flip(bit):
        return me + bit - 2 * bit * lax.rem(me // bit, 2)

    core, ex, wy = flip(1), flip(2), flip(4)
    diag = flip(2) + flip(4) - me
    low = levels // 2
    cut = lambda ref, h: ref.at[pl.ds(h * low, low)]
    part = lambda ref, h: (lambda slot: ref.at[slot, pl.ds(h * low, low)])
    whole = lambda ref: (lambda slot: ref.at[slot])
    pieces = [
        (cut(d, 0), part(gd, 0), 0),
        (cut(d, 1), part(gd, 1), 1),
        (m, whole(gm), 0),
        (x, whole(gx), 1),
        (None, whole(gel), 0),
        (None, whole(ger), 1),
        (cut(t, 0), part(gt, 0), 0),
        (cut(t, 1), part(gt, 1), 1),
    ]
    staged = {}
    for i, (src, place, _) in enumerate(pieces):
        if src is not None:
            staged[i] = pltpu.make_async_copy(src, place(me), in_sem.at[i])
            staged[i].start()

    barrier = pltpu.get_barrier_semaphore()
    for peer in (core, ex, wy):
        pl.semaphore_signal(barrier, inc=1, device_id={"gy": peer}, device_id_type=MESH)
    for peer in (east, west):
        pl.semaphore_signal(barrier, inc=1, device_id={"gx": peer}, device_id_type=MESH)
    pl.semaphore_wait(barrier, 5)

    z_copies = [
        pltpu.make_async_remote_copy(
            right, gel.at[me], z_send.at[0], z_recv.at[0],
            device_id={"gx": east}, device_id_type=MESH),
        pltpu.make_async_remote_copy(
            left, ger.at[me], z_send.at[1], z_recv.at[1],
            device_id={"gx": west}, device_id_type=MESH),
    ]
    sent = {}

    def send(i, kind, slot, peer):
        place = pieces[i][1](slot)
        copy = pltpu.make_async_remote_copy(
            place, place, send_sem.at[i, kind], recv_sem.at[i, kind],
            device_id={"gy": peer}, device_id_type=MESH)
        copy.start()
        sent[i, kind] = copy

    def give(i):
        if i in staged:
            staged[i].wait()
        else:
            z_copies[i - 4].wait_recv()
        send(i, 0, me, ex)
        send(i, 1, me, wy)
        send(i, 2, me, core)

    def relay(i):
        way = pieces[i][2]
        sent[i, 0].wait_recv()
        if way == 0:
            send(i, 3, ex, wy)
        send(i, 4, ex, core)
        sent[i, 1].wait_recv()
        if way == 1:
            send(i, 3, wy, ex)
        send(i, 5, wy, core)

    def finish(group):
        for i in group:
            sent[i, 3].wait_recv()
            send(i, 6, diag, core)
        for i in group:
            for kind in (2, 4, 5, 6):
                sent[i, kind].wait_recv()

    for i in (0, 1, 2, 3):
        give(i)
    for i in (6, 7):
        staged[i].wait()
    own = lambda ref: ref.at[me]
    pack_edges(levels, own(gd), own(gm), own(gx), own(gt), left, right)
    relay(0)
    for copy in z_copies:
        copy.start()
    relay(1)
    give(4)
    give(5)
    for i in (2, 3, 4, 5):
        relay(i)
    for i in (6, 7):
        send(i, 0, me, ex)
        send(i, 1, me, wy)
        send(i, 2, me, core)
    finish(range(6))

    def readers(j):
        return gathered_block(levels, blocks, codes, j, gd, gm, gx, gt, gel, ger)

    def physics(j, carry):
        there, grid, _, rows = readers(j)
        physics_block(
            levels, width, grid, rows[0], rows[1], there,
            grid_ref, ae.at[j], an.at[j], av.at[j], col.at[j])
        return carry

    lax.fori_loop(0, BPD, physics, 0)
    relay(6)
    relay(7)
    finish((6, 7))

    def advance(j, carry):
        _, _, tracer, rows = readers(j)

        def put(k, value):
            out[k, j] = value

        advance_block(
            levels, width, tracer, rows[2], rows[3], cur,
            ae.at[j], an.at[j], av.at[j], col.at[j], put)
        return carry

    lax.fori_loop(0, BPD, advance, 0)
    for copy in sent.values():
        copy.wait_send()
    for copy in z_copies:
        copy.wait_send()


def run_whole(count, columns, codes, density, sea, mixed, tracer):
    levels, width = density.shape[0], density.shape[-1]
    wide = width + LANES
    hbm = pl.BlockSpec(memory_space=pl.ANY)
    dma = pltpu.SemaphoreType.DMA
    f32 = lambda *shape: pltpu.VMEM(shape, jnp.float32)
    edge = (levels + 1, BPD, LANES)
    many = lambda a: pltpu.VMEM((count,) + a.shape, a.dtype)
    coefficient = f32(BPD, levels, 2 * BR, wide)
    return pl.pallas_call(
        functools.partial(whole_kernel, columns),
        in_specs=[pl.BlockSpec(memory_space=pltpu.SMEM)] + [hbm] * 4,
        out_specs=pl.BlockSpec(memory_space=pltpu.VMEM),
        out_shape=jax.ShapeDtypeStruct(tracer.shape, tracer.dtype),
        scratch_shapes=[
            many(density), many(sea), many(mixed), many(tracer),
            f32(count, *edge), f32(count, *edge), f32(*edge), f32(*edge),
            f32(levels + 2, 3 * BR, wide), f32(levels, 2 * BR, wide),
            coefficient, coefficient, coefficient, f32(BPD, 9, 2 * BR, wide),
            dma((8,)), dma((2,)), dma((2,)), dma((8, 7)), dma((8, 7)),
        ],
        compiler_params=pltpu.CompilerParams(
            collective_id=0, has_side_effects=True, vmem_limit_bytes=60 * 1024 * 1024),
        name="run_whole",
    )(codes, density, sea, mixed, tracer)


def pack_kernel(levels, d, m, x, t, left_ref, right_ref):
    pack_edges(levels, d, m, x, t, left_ref, right_ref)


def block_kernel(levels, width, blocks, codes, *refs):
    d, m, x, t = refs[0:3], refs[3:6], refs[6:9], refs[9:12]
    pel, per, tel, ter = refs[12:15], refs[15:18], refs[18:21], refs[21:24]
    out, grid_ref, cur, ae, an, av, col = refs[24:]
    j = pl.program_id(0)
    code = [codes[3 * j + o] for o in range(3)]
    there = [lax.div(c, blocks * blocks).astype(jnp.float32) for c in code]
    pat = [lax.rem(c, BPD) for c in code]
    dat = [lax.rem(lax.div(c, blocks), BPD) for c in code]

    def grid(o, k):
        if k < levels:
            return d[o][0, k, 0]
        return (m if k == levels else x)[o][0, 0].astype(jnp.float32)

    def row_of(ref, at):
        return lambda o: (lambda r: ref[o][0, r, pl.ds(at[o], 1), :])

    def put(k, value):
        out[k, 0] = value

    physics_block(
        levels, width, grid, row_of(pel, pat), row_of(per, pat), there,
        grid_ref, ae, an, av, col)
    advance_block(
        levels, width, lambda o, k: t[o][0, k, 0], row_of(tel, dat), row_of(ter, dat),
        cur, ae, an, av, col, put)


def run_parts(count, columns, codes, density, sea, mixed, tracer):
    levels, width = density.shape[0], density.shape[-1]
    blocks = count * BPD
    edge = (levels + 1, BPD, LANES)
    shape = jax.ShapeDtypeStruct(edge, jnp.float32)
    left, right = pl.pallas_call(
        functools.partial(pack_kernel, levels), out_shape=[shape, shape], name="pack_edges",
    )(density, sea, mixed, tracer)
    ring = [(i, (i + 1) % columns) for i in range(columns)]
    back = [((i + 1) % columns, i) for i in range(columns)]
    from_west = lax.ppermute(right, "gx", ring)
    from_east = lax.ppermute(left, "gx", back)
    arrays = (density, sea, mixed, tracer, from_west, from_east)
    gd, gm, gx, gt, gel, ger = (lax.all_gather(a, "gy", axis=0) for a in arrays)

    def place(which, j, pre, o):
        code = lax.rem(pre[0][3 * j + o], blocks * blocks)
        slot = lax.div(code, blocks) if which else lax.rem(code, blocks)
        return lax.div(slot, BPD), lax.rem(slot, BPD)

    def five(which, o):
        def at(j, *pre):
            dev, b = place(which, j, pre, o)
            return (dev, 0, b, 0, 0)
        return pl.BlockSpec((1, levels, 1, BR, width), at)

    def four(which, o):
        def at(j, *pre):
            return place(which, j, pre, o) + (0, 0)
        return pl.BlockSpec((1, 1, BR, width), at)

    def edges(which, o):
        def at(j, *pre):
            return (place(which, j, pre, o)[0], 0, 0, 0)
        return pl.BlockSpec((1,) + edge, at)

    three = range(3)
    specs = [five(0, o) for o in three]
    specs += [four(0, o) for o in three] * 2
    specs += [five(1, o) for o in three]
    specs += [edges(0, o) for o in three] * 2
    specs += [edges(1, o) for o in three] * 2
    wide = width + LANES
    f32 = lambda *shape: pltpu.VMEM(shape, jnp.float32)
    return pl.pallas_call(
        functools.partial(block_kernel, levels, width, blocks),
        grid_spec=pltpu.PrefetchScalarGridSpec(
            num_scalar_prefetch=1,
            grid=(BPD,),
            in_specs=specs,
            out_specs=pl.BlockSpec((levels, 1, BR, width), lambda j, *pre: (0, j, 0, 0)),
            scratch_shapes=[f32(levels + 2, 3 * BR, wide)]
            + [f32(levels, 2 * BR, wide)] * 4
            + [f32(9, 2 * BR, wide)],
        ),
        out_shape=jax.ShapeDtypeStruct(tracer.shape, tracer.dtype),
        name="run_blocks",
    )(
        codes,
        gd, gd, gd, gm, gm, gm, gx, gx, gx, gt, gt, gt,
        gel, gel, gel, ger, ger, ger, gel, gel, gel, ger, ger, ger,
    )


def plan(tile_blocks, block_owner):
    blocks = tile_blocks.shape[0]
    at = jnp.arange(blocks, dtype=jnp.int32)
    spot = jnp.arange(3 * BPD, dtype=jnp.int32)
    mine = lax.axis_index("gy") * BPD + spot // 3
    ids = jnp.sum(jnp.where(block_owner[None] == mine[:, None], tile_blocks[None], 0), axis=1)
    near = ids + spot % 3 - 1
    inside = (near >= 0) & (near < blocks)
    hit = tile_blocks[None] == jnp.clip(near, 0, blocks - 1)[:, None]
    codes = jnp.sum(jnp.where(hit, (at + blocks * block_owner)[None], 0), axis=-1)
    return codes + inside.astype(jnp.int32) * (blocks * blocks)


def on_device(count, columns, density, tracer, sea_mask, mixed_level, tile_blocks, block_owner):
    levels, height, width = density.shape
    split = lambda a: a.reshape(a.shape[:-2] + (BPD, BR, width))
    codes = plan(tile_blocks, block_owner)
    density, tracer, sea, mixed = map(split, (density, tracer, sea_mask, mixed_level))
    run = run_whole if count == 8 and columns > 2 else run_parts
    out = run(count, columns, codes, density, sea, mixed, tracer)
    return out.reshape(levels, height, width)


def solution(mesh):
    placed = (P(None, "gy", "gx"), P(None, "gy", "gx"), P("gy", "gx"), P("gy", "gx"), P(), P())
    return jax.shard_map(
        functools.partial(on_device, mesh.shape["gy"], mesh.shape["gx"]),
        mesh=mesh, in_specs=placed, out_specs=P(None, "gy", "gx"), check_vma=False,
    )
```

time: 136 us -> 114 us (0.84)
  Pallas kernels: 132 us -> 109 us
    pallas_call x3 -> x1, Pallas kernels: 132 us -> 109 us  [run_whole(): pl.pallas_call(functools.partial(whole_kernel, columns), in_specs=[pl.Blo...]
    unnamed x0 -> x5, local copies, waits for them, and re-layouts: none -> 2.92 us
where the time goes in v1:
time: 114 us; the launch traced here: 112 us
  Pallas kernels  109 us (96%)
  local copies, waits for them, and re-layouts  2.92 us (3%)
    pallas_call x1, Pallas kernels, run_whole(): pl.pallas_call(functools.partial(whole_kernel, columns), in_specs=[pl.Blo...  109 us
    unnamed x5, local copies, waits for them, and re-layouts  2.92 us

profile of v1, /device:TPU:0, one launch (start us, length us, event | category | flops | bytes accessed | tf_op | source)
XLA Modules:
  0.0 112.4 jit_solution(16202717376058630957)
XLA Ops:
  0.0 0.0 copy-start
  0.0 0.0 copy-start.1
  0.0 0.6 copy-done
  0.7 0.0 copy-done.1
  0.7 0.2 select_reduce_fusion.1
  0.9 0.2 select_reduce_fusion
  1.1 0.5 fusion.1.codes
  1.6 108.6 %run_whole.1 = f32[8,8,8,512]{3,2,1,0:T(8,128)} custom-call(s32[24]{0:T(128)} %fusion.1.codes, f32[8,8,8,512]{3,2,1,0:T(8,128)} %bitcast.6, s32[8,8,512]{2,1,0:T(8,128)} %bitcast.8, s32[8,8,512]{2,1,0:T(8,128)} %bitcast.9, f32[8,8,8,512]{3,2,1,0:T(8,128)} %bitcast.7), custom_call_target="tpu_custom_call" | custom-call | tf_op jit(solution)/shard_map/run_whole/pallas_call | solution.py:373
  110.2 2.3 %copy.8 = f32[8,64,512]{2,1,0:T(8,128)} copy(f32[8,64,512]{2,1,0:T(8,128)} %bitcast.5) | data formatting | bytes 2097152
  (3 shorter events, 0.0 us)
Async XLA Ops:
  0.0 0.7 copy-start
  0.0 0.7 copy-start.1

commit v2 on v1

--- a/solution.py
+++ b/solution.py
@@ -29,7 +29,7 @@
     return lax.broadcasted_iota(jnp.int32, (BR, LANES), 1)
 
 
-def pack_edges(levels, d, m, x, t, left_ref, right_ref):
+def pack_edges(levels, d, m, x, t, left_ref, right_ref, inner):
     lane = own_lane()
     row = lax.broadcasted_iota(jnp.int32, (BR, LANES), 0)
     end = d.shape[-1] - LANES
@@ -45,7 +45,7 @@
         span = pl.ds(start, LANES)
         tiles = [d[k, b, :, span] for k in range(levels)]
         tiles += [m[b, :, span].astype(jnp.float32), x[b, :, span].astype(jnp.float32)]
-        tiles += [t[k, b, :, span] for k in range(levels)]
+        tiles += [t(k, b, start) for k in range(levels)]
         half = LANES // 2
         for j in range(levels + 1):
             out_ref[j, pl.ds(b, 1), :] = (
@@ -54,23 +54,42 @@
     def step(b, carry):
         side(b, 0, left_ref, 0, lane < EDGE)
         side(b, end, right_ref, EDGE, lane >= LANES - EDGE)
+        if inner is not None:
+            at = (end + LANES) // 2
+            tiles = [t(k, b, at) for k in range(levels)]
+            for j in range(levels // 2):
+                inner[j, pl.ds(b, 1), :] = (
+                    one(tiles[2 * j], 0, lane < EDGE)
+                    + one(tiles[2 * j + 1], LANES // 2, lane < EDGE))
         return carry
 
     lax.fori_loop(0, BPD, step, 0)
 
 
+def spread(row, ch, to):
+    base = (ch % 2) * (LANES // 2)
+    line = jnp.broadcast_to(row(ch // 2), (BR, LANES))
+    shift = (to - base - (BR - 1) * EDGE) % LANES
+    return pltpu.roll(line, shift, 1, stride=EDGE, stride_axis=0)
+
+
+def rim_tile(lane, after, before):
+    return jnp.where(lane < EDGE, after, jnp.where(lane >= LANES - EDGE, before, 0.0))
+
+
 def edge_tile(lane, l_row, r_row, ch):
-    base = (ch % 2) * (LANES // 2)
-
-    def spread(row, to):
-        line = jnp.broadcast_to(row(ch // 2), (BR, LANES))
-        shift = (to - base - (BR - 1) * EDGE) % LANES
-        return pltpu.roll(line, shift, 1, stride=EDGE, stride_axis=0)
-
-    return jnp.where(
-        lane < EDGE,
-        spread(r_row, 0),
-        jnp.where(lane >= LANES - EDGE, spread(l_row, LANES - EDGE), 0.0),
+    return rim_tile(lane, spread(r_row, ch, 0), spread(l_row, ch, LANES - EDGE))
+
+
+def halves(value, width):
+    half = width // 2
+    first = lax.broadcasted_iota(jnp.int32, (value.shape[0], LANES), 1) < LANES // 2
+    ends = value[:, width:]
+    past = jnp.where(first, value[:, half : half + LANES], ends)
+    behind = jnp.where(first, ends, value[:, half - LANES : half])
+    return (
+        jnp.concatenate([value[:, :half], past], axis=1),
+        jnp.concatenate([value[:, half:width], behind], axis=1),
     )
 
 
@@ -82,7 +101,7 @@
     return east, west, north, south
 
 
-def physics_block(levels, width, get, l_row, r_row, there, grid_ref, ae_ref, an_ref, av_ref, col):
+def physics_block(levels, width, get, l_row, r_row, there, grid_ref, ae_ref, an_ref, av_ref, col, put):
     wide = width + LANES
     rows = 2 * BR
     rim = BR // 2
@@ -135,28 +154,28 @@
     diff = sea * (
         BASE_DIFFUSIVITY + VISBECK_ALPHA * total / (levels - mid(levels + 1)))
     for k in range(levels):
-        ae_ref[k] = ae_ref[k] * diff
-        an_ref[k] = an_ref[k] * diff
-        av_ref[k] = av_ref[k] * (0.5 * diff)
+        put(0, k, ae_ref[k] * diff)
+        put(1, k, an_ref[k] * diff)
+        put(2, k, av_ref[k] * (0.5 * diff))
     step = (0.5 * TIME_STEP) * sea
-    col[4] = (diff + east(diff)) * step * col[0]
-    col[5] = (diff + west(diff)) * step * col[1]
-    col[6] = (diff + north(diff)) * step * col[2]
-    col[7] = (diff + south(diff)) * step * col[3]
-    col[8] = step
-
-
-def advance_block(levels, width, get, l_row, r_row, cur, ae_ref, an_ref, av_ref, col, put):
-    wide = width + LANES
+    for i in range(4):
+        put(3, i, col[i])
+    put(3, 4, (diff + east(diff)) * step * col[0])
+    put(3, 5, (diff + west(diff)) * step * col[1])
+    put(3, 6, (diff + north(diff)) * step * col[2])
+    put(3, 7, (diff + south(diff)) * step * col[3])
+    put(3, 8, step)
+
+
+def advance_block(levels, half, get, tile_of, cur, ae_ref, an_ref, av_ref, col, put):
+    wide = half + LANES
     rows = 2 * BR
     rim = BR // 2
-    lane = own_lane()
     for o in range(3):
         first, size, at = ((rim, rim, 0), (0, BR, rim), (0, rim, rim + BR))[o]
         for k in range(levels):
-            cur[k, at : at + size, :width] = get(o, k)[first : first + size]
-            tile = edge_tile(lane, l_row(o), r_row(o), levels + 2 + k)
-            cur[k, at : at + size, width:] = tile[first : first + size]
+            cur[k, at : at + size, :half] = get(o, k)[first : first + size]
+            cur[k, at : at + size, half:] = tile_of(o, k)[first : first + size]
     east, west, north, south = shifts(rows, wide)
 
     def iterate(_, carry):
@@ -185,10 +204,10 @@
 
     lax.fori_loop(0, ITERS, iterate, 0)
     for k in range(levels):
-        put(k, cur[k, rim : rim + BR, :width])
-
-
-def gathered_block(levels, blocks, codes, j, gd, gm, gx, gt, gel, ger):
+        put(k, cur[k, rim : rim + BR, :half])
+
+
+def gathered_block(levels, blocks, codes, j, gd, gm, gx, gts, gel, ger, gin):
     code = [codes[3 * j + o] for o in range(3)]
     pair = [lax.rem(c, blocks * blocks) for c in code]
     there = [lax.div(c, blocks * blocks).astype(jnp.float32) for c in code]
@@ -205,21 +224,37 @@
             return gd[dev, k, at]
         return (gm if k == levels else gx)[dev, at].astype(jnp.float32)
 
-    def tracer(o, k):
-        dev, at = dyn[o]
-        return gt[dev, k, at]
+    def tracer(part):
+        def get(o, k):
+            dev, at = dyn[o]
+            return gts[part][dev, k, at]
+        return get
 
     def row_of(ref, places):
         return lambda o: (lambda r: ref[places[o][0], r, pl.ds(places[o][1], 1), :])
 
-    rows = [row_of(ref, places) for places in (phys, dyn) for ref in (gel, ger)]
-    return there, grid, tracer, rows
+    lane = own_lane()
+    l_row, r_row, i_row = (row_of(ref, dyn) for ref in (gel, ger, gin))
+
+    def tile(part):
+        def get(o, k):
+            ch = levels + 2 + k
+            if part == 0:
+                after, before = spread(i_row(o), k, 0), spread(l_row(o), ch, LANES - EDGE)
+            else:
+                dev, at = dyn[o]
+                end = gts[0].shape[-1]
+                after, before = spread(r_row(o), ch, 0), gts[0][dev, k, at, :, end - LANES :]
+            return rim_tile(lane, after, before)
+        return get
+
+    return there, grid, row_of(gel, phys), row_of(ger, phys), tracer, tile
 
 
 def whole_kernel(
     columns, codes, d, m, x, t, out,
-    gd, gm, gx, gt, gel, ger, left, right,
-    grid_ref, cur, ae, an, av, col,
+    gd, gm, gx, gt0, gt1, gel, ger, gin, left, right,
+    grid_ref, cur, raw_e, raw_n, raw_v, raw_c, ae, an, av, col,
     in_sem, z_send, z_recv, send_sem, recv_sem,
 ):
     levels, width = d.shape[0], d.shape[-1]
@@ -239,6 +274,8 @@
     cut = lambda ref, h: ref.at[pl.ds(h * low, low)]
     part = lambda ref, h: (lambda slot: ref.at[slot, pl.ds(h * low, low)])
     whole = lambda ref: (lambda slot: ref.at[slot])
+    half = width // 2
+    side = lambda h, p: t.at[pl.ds(h * low, low), :, :, pl.ds(p * half, half)]
     pieces = [
         (cut(d, 0), part(gd, 0), 0),
         (cut(d, 1), part(gd, 1), 1),
@@ -246,9 +283,13 @@
         (x, whole(gx), 1),
         (None, whole(gel), 0),
         (None, whole(ger), 1),
-        (cut(t, 0), part(gt, 0), 0),
-        (cut(t, 1), part(gt, 1), 1),
+        (None, whole(gin), 0),
+        (side(0, 0), part(gt0, 0), 0),
+        (side(1, 0), part(gt0, 1), 1),
+        (side(0, 1), part(gt1, 0), 0),
+        (side(1, 1), part(gt1, 1), 1),
     ]
+    near, far = (7, 8), (9, 10)
     staged = {}
     for i, (src, place, _) in enumerate(pieces):
         if src is not None:
@@ -281,10 +322,6 @@
         sent[i, kind] = copy
 
     def give(i):
-        if i in staged:
-            staged[i].wait()
-        else:
-            z_copies[i - 4].wait_recv()
         send(i, 0, me, ex)
         send(i, 1, me, wy)
         send(i, 2, me, core)
@@ -309,52 +346,73 @@
                 sent[i, kind].wait_recv()
 
     for i in (0, 1, 2, 3):
+        staged[i].wait()
         give(i)
-    for i in (6, 7):
+    for i in near + far:
         staged[i].wait()
     own = lambda ref: ref.at[me]
-    pack_edges(levels, own(gd), own(gm), own(gx), own(gt), left, right)
+
+    def own_tracer(k, b, start):
+        ref = gt0 if start < half else gt1
+        return ref[me, k, b, :, pl.ds(start % half, LANES)]
+
+    pack_edges(levels, own(gd), own(gm), own(gx), own_tracer, left, right, own(gin))
     relay(0)
     for copy in z_copies:
         copy.start()
+    give(6)
     relay(1)
-    give(4)
-    give(5)
-    for i in (2, 3, 4, 5):
+    for i in (4, 5):
+        z_copies[i - 4].wait_recv()
+        give(i)
+    for i in (2, 3, 6, 4, 5):
         relay(i)
-    for i in (6, 7):
-        send(i, 0, me, ex)
-        send(i, 1, me, wy)
-        send(i, 2, me, core)
-    finish(range(6))
+    for i in near:
+        give(i)
+    finish(range(7))
 
     def readers(j):
-        return gathered_block(levels, blocks, codes, j, gd, gm, gx, gt, gel, ger)
+        return gathered_block(
+            levels, blocks, codes, j, gd, gm, gx, (gt0, gt1), gel, ger, gin)
 
     def physics(j, carry):
-        there, grid, _, rows = readers(j)
+        there, grid, l_row, r_row, _, _ = readers(j)
+
+        def put(which, k, value):
+            for p, piece in enumerate(halves(value, width)):
+                (ae, an, av, col)[which][p, j, k] = piece
+
         physics_block(
-            levels, width, grid, rows[0], rows[1], there,
-            grid_ref, ae.at[j], an.at[j], av.at[j], col.at[j])
+            levels, width, grid, l_row, r_row, there,
+            grid_ref, raw_e, raw_n, raw_v, raw_c, put)
         return carry
 
+    def advance(p):
+        def step(j, carry):
+            _, _, _, _, tracer, tile = readers(j)
+
+            def put(k, value):
+                out[k, j, :, p * half : (p + 1) * half] = value
+
+            advance_block(
+                levels, half, tracer(p), tile(p), cur,
+                ae.at[p, j], an.at[p, j], av.at[p, j], col.at[p, j], put)
+            return carry
+        return step
+
     lax.fori_loop(0, BPD, physics, 0)
-    relay(6)
-    relay(7)
-    finish((6, 7))
-
-    def advance(j, carry):
-        _, _, tracer, rows = readers(j)
-
-        def put(k, value):
-            out[k, j] = value
-
-        advance_block(
-            levels, width, tracer, rows[2], rows[3], cur,
-            ae.at[j], an.at[j], av.at[j], col.at[j], put)
-        return carry
-
-    lax.fori_loop(0, BPD, advance, 0)
+    for i in near:
+        relay(i)
+    for i in far:
+        give(i)
+    finish(near)
+    pause = BPD * 3 // 4
+    lax.fori_loop(0, pause, advance(0), 0)
+    for i in far:
+        relay(i)
+    lax.fori_loop(pause, BPD, advance(0), 0)
+    finish(far)
+    lax.fori_loop(0, BPD, advance(1), 0)
     for copy in sent.values():
         copy.wait_send()
     for copy in z_copies:
@@ -369,18 +427,22 @@
     f32 = lambda *shape: pltpu.VMEM(shape, jnp.float32)
     edge = (levels + 1, BPD, LANES)
     many = lambda a: pltpu.VMEM((count,) + a.shape, a.dtype)
-    coefficient = f32(BPD, levels, 2 * BR, wide)
+    slim = width // 2 + LANES
+    coefficient = f32(2, BPD, levels, 2 * BR, slim)
+    many_half = pltpu.VMEM((count,) + tracer.shape[:-1] + (width // 2,), tracer.dtype)
     return pl.pallas_call(
         functools.partial(whole_kernel, columns),
         in_specs=[pl.BlockSpec(memory_space=pltpu.SMEM)] + [hbm] * 4,
         out_specs=pl.BlockSpec(memory_space=pltpu.VMEM),
         out_shape=jax.ShapeDtypeStruct(tracer.shape, tracer.dtype),
         scratch_shapes=[
-            many(density), many(sea), many(mixed), many(tracer),
-            f32(count, *edge), f32(count, *edge), f32(*edge), f32(*edge),
-            f32(levels + 2, 3 * BR, wide), f32(levels, 2 * BR, wide),
-            coefficient, coefficient, coefficient, f32(BPD, 9, 2 * BR, wide),
-            dma((8,)), dma((2,)), dma((2,)), dma((8, 7)), dma((8, 7)),
+            many(density), many(sea), many(mixed), many_half, many_half,
+            f32(count, *edge), f32(count, *edge), f32(count, levels // 2, BPD, LANES),
+            f32(*edge), f32(*edge),
+            f32(levels + 2, 3 * BR, wide), f32(levels, 2 * BR, slim),
+            *[f32(levels, 2 * BR, wide)] * 3, f32(5, 2 * BR, wide),
+            *[coefficient] * 3, f32(2, BPD, 9, 2 * BR, slim),
+            dma((11,)), dma((2,)), dma((2,)), dma((11, 7)), dma((11, 7)),
         ],
         compiler_params=pltpu.CompilerParams(
             collective_id=0, has_side_effects=True, vmem_limit_bytes=60 * 1024 * 1024),
@@ -389,13 +451,16 @@
 
 
 def pack_kernel(levels, d, m, x, t, left_ref, right_ref):
-    pack_edges(levels, d, m, x, t, left_ref, right_ref)
+    def tracer(k, b, start):
+        return t[k, b, :, pl.ds(start, LANES)]
+
+    pack_edges(levels, d, m, x, tracer, left_ref, right_ref, None)
 
 
 def block_kernel(levels, width, blocks, codes, *refs):
     d, m, x, t = refs[0:3], refs[3:6], refs[6:9], refs[9:12]
     pel, per, tel, ter = refs[12:15], refs[15:18], refs[18:21], refs[21:24]
-    out, grid_ref, cur, ae, an, av, col = refs[24:]
+    out, grid_ref, cur, raw_e, raw_n, raw_v, raw_c, ae, an, av, col = refs[24:]
     j = pl.program_id(0)
     code = [codes[3 * j + o] for o in range(3)]
     there = [lax.div(c, blocks * blocks).astype(jnp.float32) for c in code]
@@ -410,15 +475,34 @@
     def row_of(ref, at):
         return lambda o: (lambda r: ref[o][0, r, pl.ds(at[o], 1), :])
 
-    def put(k, value):
-        out[k, 0] = value
-
+    def put_parts(which, k, value):
+        for p, piece in enumerate(halves(value, width)):
+            (ae, an, av, col)[which][p, k] = piece
+
+    half = width // 2
     physics_block(
         levels, width, grid, row_of(pel, pat), row_of(per, pat), there,
-        grid_ref, ae, an, av, col)
-    advance_block(
-        levels, width, lambda o, k: t[o][0, k, 0], row_of(tel, dat), row_of(ter, dat),
-        cur, ae, an, av, col, put)
+        grid_ref, raw_e, raw_n, raw_v, raw_c, put_parts)
+    lane = own_lane()
+    l_row, r_row = row_of(tel, dat), row_of(ter, dat)
+
+    for p in range(2):
+        def get(o, k, p=p):
+            return t[o][0, k, 0, :, p * half : (p + 1) * half]
+
+        def tile(o, k, p=p):
+            ch = levels + 2 + k
+            if p == 0:
+                after = t[o][0, k, 0, :, half : half + LANES]
+                return rim_tile(lane, after, spread(l_row(o), ch, LANES - EDGE))
+            before = t[o][0, k, 0, :, half - LANES : half]
+            return rim_tile(lane, spread(r_row(o), ch, 0), before)
+
+        def put(k, value, p=p):
+            out[k, 0, :, p * half : (p + 1) * half] = value
+
+        advance_block(
+            levels, half, get, tile, cur, ae.at[p], an.at[p], av.at[p], col.at[p], put)
 
 
 def run_parts(count, columns, codes, density, sea, mixed, tracer):
@@ -458,6 +542,7 @@
         return pl.BlockSpec((1,) + edge, at)
 
     three = range(3)
+    slim = width // 2 + LANES
     specs = [five(0, o) for o in three]
     specs += [four(0, o) for o in three] * 2
     specs += [five(1, o) for o in three]
@@ -472,9 +557,11 @@
             grid=(BPD,),
             in_specs=specs,
             out_specs=pl.BlockSpec((levels, 1, BR, width), lambda j, *pre: (0, j, 0, 0)),
-            scratch_shapes=[f32(levels + 2, 3 * BR, wide)]
-            + [f32(levels, 2 * BR, wide)] * 4
-            + [f32(9, 2 * BR, wide)],
+            scratch_shapes=[f32(levels + 2, 3 * BR, wide), f32(levels, 2 * BR, slim)]
+            + [f32(levels, 2 * BR, wide)] * 3
+            + [f32(5, 2 * BR, wide)]
+            + [f32(2, levels, 2 * BR, slim)] * 3
+            + [f32(2, 9, 2 * BR, slim)],
         ),
         out_shape=jax.ShapeDtypeStruct(tracer.shape, tracer.dtype),
         name="run_blocks",

time: 114 us -> 111 us (0.974); the launches traced: 112 us -> 111 us
  Pallas kernels: 109 us -> 107 us
    pallas_call x1, Pallas kernels: 109 us -> 107 us  [run_whole(): pl.pallas_call(functools.partial(whole_kernel, columns), in_specs=[pl.Blo...]
where the time goes in v2:
time: 111 us
  Pallas kernels  107 us (96%)
  local copies, waits for them, and re-layouts  2.92 us (3%)
    pallas_call x1, Pallas kernels, run_whole(): pl.pallas_call(functools.partial(whole_kernel, columns), in_specs=[pl.Blo...  107 us
    unnamed x5, local copies, waits for them, and re-layouts  2.92 us

profile of v2, /device:TPU:0, one launch (start us, length us, event | category | flops | bytes accessed | tf_op | source)
XLA Modules:
  0.0 110.9 jit_solution(18403018049899341510)
XLA Ops:
  0.0 0.0 copy-start
  0.0 0.0 copy-start.1
  0.0 0.6 copy-done
  0.7 0.0 copy-done.1
  0.7 0.2 select_reduce_fusion.1
  0.9 0.2 select_reduce_fusion
  1.1 0.5 fusion.1.codes
  1.6 107.1 %run_whole.1 = f32[8,8,8,512]{3,2,1,0:T(8,128)} custom-call(s32[24]{0:T(128)} %fusion.1.codes, f32[8,8,8,512]{3,2,1,0:T(8,128)} %bitcast.6, s32[8,8,512]{2,1,0:T(8,128)} %bitcast.8, s32[8,8,512]{2,1,0:T(8,128)} %bitcast.9, f32[8,8,8,512]{3,2,1,0:T(8,128)} %bitcast.7), custom_call_target="tpu_custom_call" | custom-call | tf_op jit(solution)/shard_map/run_whole/pallas_call | solution.py:433
  108.7 2.3 %copy.8 = f32[8,64,512]{2,1,0:T(8,128)} copy(f32[8,64,512]{2,1,0:T(8,128)} %bitcast.5) | data formatting | bytes 2097152
  (3 shorter events, 0.0 us)
Async XLA Ops:
  0.0 0.7 copy-start
  0.0 0.7 copy-start.1

commit v3 on v2

--- a/solution.py
+++ b/solution.py
@@ -400,17 +400,20 @@
             return carry
         return step
 
-    lax.fori_loop(0, BPD, physics, 0)
-    for i in near:
-        relay(i)
+    half_way, late = BPD // 2, BPD * 3 // 4
+    lax.fori_loop(0, half_way, physics, 0)
+    relay(near[0])
+    lax.fori_loop(half_way, late, physics, 0)
+    relay(near[1])
     for i in far:
         give(i)
+    lax.fori_loop(late, BPD, physics, 0)
     finish(near)
-    pause = BPD * 3 // 4
-    lax.fori_loop(0, pause, advance(0), 0)
-    for i in far:
-        relay(i)
-    lax.fori_loop(pause, BPD, advance(0), 0)
+    lax.fori_loop(0, half_way, advance(0), 0)
+    relay(far[0])
+    lax.fori_loop(half_way, late, advance(0), 0)
+    relay(far[1])
+    lax.fori_loop(late, BPD, advance(0), 0)
     finish(far)
     lax.fori_loop(0, BPD, advance(1), 0)
     for copy in sent.values():

time: 111 us -> 111 us (level)
  no operation moved by 1% of the time
where the time goes in v3:
time: 111 us
  Pallas kernels  107 us (96%)
  local copies, waits for them, and re-layouts  2.92 us (3%)
    pallas_call x1, Pallas kernels, run_whole(): pl.pallas_call(functools.partial(whole_kernel, columns), in_specs=[pl.Blo...  107 us
    unnamed x5, local copies, waits for them, and re-layouts  2.92 us

profile of v3, /device:TPU:0, one launch (start us, length us, event | category | flops | bytes accessed | tf_op | source)
XLA Modules:
  0.0 110.6 jit_solution(2035507636178588327)
XLA Ops:
  0.0 0.0 copy-start
  0.0 0.0 copy-start.1
  0.0 0.6 copy-done
  0.7 0.0 copy-done.1
  0.7 0.2 select_reduce_fusion.1
  0.9 0.2 select_reduce_fusion
  1.1 0.5 fusion.1.codes
  1.6 106.8 %run_whole.1 = f32[8,8,8,512]{3,2,1,0:T(8,128)} custom-call(s32[24]{0:T(128)} %fusion.1.codes, f32[8,8,8,512]{3,2,1,0:T(8,128)} %bitcast.6, s32[8,8,512]{2,1,0:T(8,128)} %bitcast.8, s32[8,8,512]{2,1,0:T(8,128)} %bitcast.9, f32[8,8,8,512]{3,2,1,0:T(8,128)} %bitcast.7), custom_call_target="tpu_custom_call" | custom-call | tf_op jit(solution)/shard_map/run_whole/pallas_call | solution.py:436
  108.4 2.3 %copy.8 = f32[8,64,512]{2,1,0:T(8,128)} copy(f32[8,64,512]{2,1,0:T(8,128)} %bitcast.5) | data formatting | bytes 2097152
  (3 shorter events, 0.0 us)
Async XLA Ops:
  0.0 0.7 copy-start
  0.0 0.7 copy-start.1
